TPU v7x, 128 devices: a whole 4x4x4 slice. The times are simulated.
128 devices in a mesh: outer: 8 (over z, x_lo), inner: 16 (over y, x_hi, core).
Axes of the slice: x: 4 (x_hi: 2, x_lo: 2; x = x_hi * 2 + x_lo), y: 4, z: 4, core: 2. Of those that a mesh axis runs over, the one named last changes fastest.
Arguments:
- query_proj: bfloat16 [8192, 8192], P(('outer', 'inner')), may hold values from -8 to 8
- key_proj: bfloat16 [8192, 512], P(('outer', 'inner')), may hold values from -8 to 8
- value_proj: bfloat16 [8192, 512], P(('outer', 'inner')), may hold values from -6 to 6
- positions: int32 [8192], P(('outer', 'inner')), may hold values from 0 to 8191, each once
Outputs:
- attended: bfloat16 [8192, 8192], P(('outer', 'inner'))
Inputs may be any that keep to these rules, and one draw needn't show every extreme that they name: `positions`: each position from 0 to 8191 appears exactly once.
All inputs are finite; a program needn't handle non-finite values.
Results may differ from a plain program's by a relative error of at most 0.005.
Values may be sent and summed in bfloat16 or wider, within the bound.
No kernel may reach another device: no remote copies, remote signals or barrier semaphores. Data moves between devices by JAX's collectives and lax.ppermute only.
A program may use at most 64 MiB of HBM per device.

v0:
```python
import math

import jax
import jax.numpy as jnp
from jax import lax
from jax.sharding import Mesh
from jax.sharding import PartitionSpec as P

HEAD_WIDTH = 128
OUTER = ("outer_0", "outer_1")
OUTER_INNER = ("outer_0", "outer_1", "inner")


masked_score = -1e30


def laid_out(parts, dim):
    dims = list(parts.shape[1:])
    dims[dim] *= parts.shape[0]
    return jnp.moveaxis(parts, 0, dim).reshape(dims)


def sent_to_all(value, axis):
    peers = lax.axis_size(axis)
    return lax.all_to_all(
        jnp.broadcast_to(value[None], (peers, *value.shape)), axis, 0, 0, tiled=True
    )


def gather_directly(value, axis, dim):
    return laid_out(sent_to_all(value, axis), dim)


def gather_axes(value, axes, dim):
    for axis in reversed(axes):
        value = lax.all_gather(value, axis, axis=dim, tiled=True)
    return value


def update(carried, key_value_block, key_pos, query_cluster, query_pos):
    running_top, running_sum, accumulated = carried
    heads_kv = query_cluster.shape[0]
    head_dim = query_cluster.shape[2]
    width = heads_kv * head_dim
    rows_kv = key_value_block.shape[0]
    key_slice = key_value_block[:, :width].reshape(rows_kv, heads_kv, head_dim)
    value_slice = key_value_block[:, width:].reshape(rows_kv, heads_kv, head_dim)
    scores = jnp.einsum(
        "lva,vga->vlg", key_slice, query_cluster, preferred_element_type=jnp.float32
    ) * (1.0 / math.sqrt(head_dim))
    visible = key_pos[None, :, None] <= query_pos[None, None, :]
    block_top = jnp.max(jnp.where(visible, scores, masked_score), axis=1)
    new_top = jnp.maximum(running_top, block_top)
    softmax_weights = jnp.where(visible, jnp.exp(scores - new_top[:, None, :]), 0.0)
    rescale = jnp.exp(running_top - new_top)
    running_sum = running_sum * rescale + jnp.sum(softmax_weights, axis=1)
    accumulated = accumulated * rescale[:, :, None] + jnp.einsum(
        "goi,ogt->git",
        softmax_weights.astype(jnp.bfloat16),
        value_slice,
        preferred_element_type=jnp.float32,
    )
    return (new_top, running_sum, accumulated)


def make_folder(query_cluster, query_pos):

    def fold_piece(carried, kv_piece, first_row):
        kv_rows, key_pos = kv_piece
        row_count = kv_rows.shape[0]
        sub_rows = math.gcd(row_count, 512)
        stacked = kv_rows.reshape(row_count // sub_rows, sub_rows, kv_rows.shape[1])
        pos_stack = key_pos.reshape(row_count // sub_rows, sub_rows)

        def inner_step(carry_in, sub_block):
            return (update(carry_in, sub_block[0], sub_block[1], query_cluster, query_pos), None)

        carried, unused = lax.scan(inner_step, carried, (stacked, pos_stack))
        return carried

    return fold_piece


def start_state(heads_kv, query_rows, head_dim):
    return (
        jnp.full((heads_kv, query_rows), masked_score, jnp.float32),
        jnp.zeros((heads_kv, query_rows), jnp.float32),
        jnp.zeros((heads_kv, query_rows, head_dim), jnp.float32),
    )


def finish(carried):
    return carried[2] / carried[1][:, :, None]


def body(query_proj, key_proj, value_proj, positions):
    tok_rows = query_proj.shape[0]
    head_dim = HEAD_WIDTH
    heads_all = query_proj.shape[1] // head_dim
    heads_kv = key_proj.shape[1] // head_dim
    group_size = heads_all // heads_kv
    inner_count = lax.axis_size("inner")
    per_device = heads_all // inner_count
    repeat_count = group_size // per_device
    key_spread = jnp.repeat(key_proj.reshape(tok_rows, heads_kv, head_dim), repeat_count, axis=1)
    value_broadcast = jnp.repeat(
        value_proj.reshape(tok_rows, heads_kv, head_dim), repeat_count, axis=1
    )
    kv_spread = jnp.concatenate([key_spread, value_broadcast], axis=2).reshape(
        tok_rows, inner_count * 2 * head_dim
    )
    query_heads, kv_heads = (
        lax.all_to_all(query_proj, "inner", split_axis=1, concat_axis=0, tiled=True),
        lax.all_to_all(kv_spread, "inner", split_axis=1, concat_axis=0, tiled=True),
    )
    group_pos = gather_directly(positions, "inner", 0)
    group_rows = query_heads.shape[0]
    query_cluster = (
        query_heads.reshape(group_rows, per_device, head_dim)
        .transpose(1, 0, 2)
        .reshape(1, per_device * group_rows, head_dim)
    )
    query_pos = jnp.tile(group_pos, per_device)
    folder = make_folder(query_cluster, query_pos)
    initial = start_state(1, per_device * group_rows, head_dim)
    carried = folder(
        initial, (gather_axes(kv_heads, OUTER, 0), gather_axes(group_pos, OUTER, 0)), jnp.int32(0)
    )
    result = (
        finish(carried)
        .reshape(per_device, group_rows, head_dim)
        .transpose(1, 0, 2)
        .reshape(group_rows, per_device * head_dim)
        .astype(jnp.bfloat16)
    )
    return lax.all_to_all(result, "inner", split_axis=0, concat_axis=1, tiled=True)


def solution(mesh):
    finer = Mesh(mesh.devices.reshape(4, 2, mesh.shape["inner"]), ("outer_0", "outer_1", "inner"))
    return jax.shard_map(
        body,
        mesh=finer,
        in_specs=(P(OUTER_INNER, None), P(OUTER_INNER, None), P(OUTER_INNER, None), P(OUTER_INNER)),
        out_specs=P(OUTER_INNER, None),
        check_vma=False,
    )
```

profile of v0, /device:TPU:1, one launch (start us, length us, event | category | flops | bytes accessed | tf_op | source)
XLA Modules:
  0.0 281.3 jit_solution(1181417575358874102)
XLA Ops:
  8.4 19.5 %all_to_all.54 = bf16[64,16,256]{2,0,1:T(8,128)(2,1)} all-to-all(bf16[64,16,256]{2,0,1:T(8,128)(2,1)S(1)} %pad_maximum_fusion), channel_id=1, replica_groups=mesh['outer_0'=4,'outer_1'=2,'inner'=16] {'inner'}, dimensions={1} | all-to-all | bytes 1048576 | tf_op jit(solution)/shard_map/all_to_all | solution.py:114
  28.0 22.0 %all-gather.3.cloned.1.call-done = bf16[2048,256]{1,0:T(8,128)(2,1)} async-done(((bf16[1024,256]{1,0:T(8,128)(2,1)}), bf16[2048,256]{1,0:T(8,128)(2,1)}) %all-gather.3.cloned.1.call-update) | async-done | bytes 1048592 | tf_op jit(solution)/shard_map/all_gather | solution.py:36
  51.3 7.3 %all-to-all-start = ((s32[16,1,64]{2,1,0:T(1,128)}), s32[16,1,64]{2,1,0:T(1,128)S(1)}, u32[]{:S(2)}, u32[]{:S(2)}) async-start(s32[16,1,64]{2,1,0:T(1,128)} %broadcast_in_dim.35), calls=%async_computation | async-start | bytes 16384 | tf_op jit(solution)/shard_map/all_to_all | solution.py:25
  60.8 4.7 %all-to-all-done = s32[16,1,64]{2,1,0:T(1,128)S(1)} async-done(((s32[16,1,64]{2,1,0:T(1,128)}), s32[16,1,64]{2,1,0:T(1,128)S(1)}, u32[]{:S(2)}, u32[]{:S(2)}) %all-to-all-start) | async-done | bytes 4128 | tf_op jit(solution)/shard_map/all_to_all | solution.py:25
  65.5 4.0 %all-to-all-start.2 = ((bf16[64,16,512]{2,0,1:T(8,128)(2,1)}), bf16[64,16,512]{2,0,1:T(8,128)(2,1)S(1)}, u32[]{:S(2)}, u32[]{:S(2)}) async-start(bf16[64,16,512]{2,0,1:T(8,128)(2,1)} %bitcast.50), calls=%async_computation.2 | async-start | bytes 2097152 | tf_op jit(solution)/shard_map/all_to_all | solution.py:113
  70.7 11.4 %all_gather.12 = s32[2048]{0:T(1024)S(1)} all-gather(s32[1024]{0:T(1024)S(1)} %reshape.91), channel_id=1, replica_groups=mesh['outer_0'=4,'outer_1'=2,'inner'=16] {'outer_1'}, dimensions={0}, use_global_device_ids=true | all-gather | bytes 12288 | tf_op jit(solution)/shard_map/all_gather | solution.py:36
  82.0 11.1 %all_gather.13 = s32[8192]{0:T(1024)S(1)} all-gather(s32[2048]{0:T(1024)S(1)} %all_gather.12), channel_id=1, replica_groups=mesh['outer_0'=4,'outer_1'=2,'inner'=16] {'outer_0'}, dimensions={0}, use_global_device_ids=true | all-gather | bytes 40960 | tf_op jit(solution)/shard_map/all_gather | solution.py:36
  93.6 7.8 %all-gather.5.cloned.1.call-done = bf16[8192,256]{1,0:T(8,128)(2,1)} async-done(((bf16[2048,256]{1,0:T(8,128)(2,1)}), bf16[8192,256]{1,0:T(8,128)(2,1)}) %all-gather.5.cloned.1.call-update) | async-done | bytes 4194320 | tf_op jit(solution)/shard_map/all_gather | solution.py:36
  101.3 144.7 %while.15 = (s32[]{:T(128)}, f32[1,4096]{1,0:T(1,128)S(1)}, f32[1,4096]{1,0:T(1,128)S(1)}, f32[1,4096,128]{2,1,0:T(8,128)}, s32[16,512]{1,0:T(8,128)S(1)}, /*ind...) while((s32[]{:T(128)}, f32[1,4096]{1,0:T(1,128)S(1)}, ...), condition=%wide.region_3.4_spmd.clone, body=%wide.region_0.3_spmd.clone.sunk | while | flops 1104695296 | bytes 48347320 | solution.py:78
  106.1 3.0 %fusion.35 = f32[1,4096,128]{2,1,0:T(8,128)S(1)} fusion(f32[512,4096]{1,0:T(8,128)S(1)} %get-tuple-element.154, f32[4096]{0:T(1024)S(1)} %bitcast.73, s32[4096]{0:T(1024)S(1)} %bitcast.82, s32[512]{0:T(512)S(1)} %bitcast.94, f32[1,4096,128]{2,1,0:T(8,128)S(1)} %copy-done.1, f32[4096]{0:T(1024)S(1)} %bitcast.91, pred[]{:T(512)S(6)} %compare.3, ...), kind=kOutput, calls=%fused_computation.7.clone.1 | convolution fusion | flops 548929536 | bytes 12765185 | tf_op jit(solution)/shard_map/while/body/eval_jaxpr/goi,ogt->git/dot_general | solution.py:57
  124.2 3.0 %fusion.35 = f32[1,4096,128]{2,1,0:T(8,128)S(1)} fusion(f32[512,4096]{1,0:T(8,128)S(1)} %get-tuple-element.154, f32[4096]{0:T(1024)S(1)} %bitcast.73, s32[4096]{0:T(1024)S(1)} %bitcast.82, s32[512]{0:T(512)S(1)} %bitcast.94, f32[1,4096,128]{2,1,0:T(8,128)S(1)} %copy-done.1, f32[4096]{0:T(1024)S(1)} %bitcast.91, pred[]{:T(512)S(6)} %compare.3, ...), kind=kOutput, calls=%fused_computation.7.clone.1 | convolution fusion | flops 548929536 | bytes 12765185 | tf_op jit(solution)/shard_map/while/body/eval_jaxpr/goi,ogt->git/dot_general | solution.py:57
  133.2 3.0 %fusion.35 = f32[1,4096,128]{2,1,0:T(8,128)S(1)} fusion(f32[512,4096]{1,0:T(8,128)S(1)} %get-tuple-element.154, f32[4096]{0:T(1024)S(1)} %bitcast.73, s32[4096]{0:T(1024)S(1)} %bitcast.82, s32[512]{0:T(512)S(1)} %bitcast.94, f32[1,4096,128]{2,1,0:T(8,128)S(1)} %copy-done.1, f32[4096]{0:T(1024)S(1)} %bitcast.91, pred[]{:T(512)S(6)} %compare.3, ...), kind=kOutput, calls=%fused_computation.7.clone.1 | convolution fusion | flops 548929536 | bytes 12765185 | tf_op jit(solution)/shard_map/while/body/eval_jaxpr/goi,ogt->git/dot_general | solution.py:57
  142.3 3.0 %fusion.35 = f32[1,4096,128]{2,1,0:T(8,128)S(1)} fusion(f32[512,4096]{1,0:T(8,128)S(1)} %get-tuple-element.154, f32[4096]{0:T(1024)S(1)} %bitcast.73, s32[4096]{0:T(1024)S(1)} %bitcast.82, s32[512]{0:T(512)S(1)} %bitcast.94, f32[1,4096,128]{2,1,0:T(8,128)S(1)} %copy-done.1, f32[4096]{0:T(1024)S(1)} %bitcast.91, pred[]{:T(512)S(6)} %compare.3, ...), kind=kOutput, calls=%fused_computation.7.clone.1 | convolution fusion | flops 548929536 | bytes 12765185 | tf_op jit(solution)/shard_map/while/body/eval_jaxpr/goi,ogt->git/dot_general | solution.py:57
  151.3 3.0 %fusion.35 = f32[1,4096,128]{2,1,0:T(8,128)S(1)} fusion(f32[512,4096]{1,0:T(8,128)S(1)} %get-tuple-element.154, f32[4096]{0:T(1024)S(1)} %bitcast.73, s32[4096]{0:T(1024)S(1)} %bitcast.82, s32[512]{0:T(512)S(1)} %bitcast.94, f32[1,4096,128]{2,1,0:T(8,128)S(1)} %copy-done.1, f32[4096]{0:T(1024)S(1)} %bitcast.91, pred[]{:T(512)S(6)} %compare.3, ...), kind=kOutput, calls=%fused_computation.7.clone.1 | convolution fusion | flops 548929536 | bytes 12765185 | tf_op jit(solution)/shard_map/while/body/eval_jaxpr/goi,ogt->git/dot_general | solution.py:57
  160.4 3.0 %fusion.35 = f32[1,4096,128]{2,1,0:T(8,128)S(1)} fusion(f32[512,4096]{1,0:T(8,128)S(1)} %get-tuple-element.154, f32[4096]{0:T(1024)S(1)} %bitcast.73, s32[4096]{0:T(1024)S(1)} %bitcast.82, s32[512]{0:T(512)S(1)} %bitcast.94, f32[1,4096,128]{2,1,0:T(8,128)S(1)} %copy-done.1, f32[4096]{0:T(1024)S(1)} %bitcast.91, pred[]{:T(512)S(6)} %compare.3, ...), kind=kOutput, calls=%fused_computation.7.clone.1 | convolution fusion | flops 548929536 | bytes 12765185 | tf_op jit(solution)/shard_map/while/body/eval_jaxpr/goi,ogt->git/dot_general | solution.py:57
  169.4 3.0 %fusion.35 = f32[1,4096,128]{2,1,0:T(8,128)S(1)} fusion(f32[512,4096]{1,0:T(8,128)S(1)} %get-tuple-element.154, f32[4096]{0:T(1024)S(1)} %bitcast.73, s32[4096]{0:T(1024)S(1)} %bitcast.82, s32[512]{0:T(512)S(1)} %bitcast.94, f32[1,4096,128]{2,1,0:T(8,128)S(1)} %copy-done.1, f32[4096]{0:T(1024)S(1)} %bitcast.91, pred[]{:T(512)S(6)} %compare.3, ...), kind=kOutput, calls=%fused_computation.7.clone.1 | convolution fusion | flops 548929536 | bytes 12765185 | tf_op jit(solution)/shard_map/while/body/eval_jaxpr/goi,ogt->git/dot_general | solution.py:57
  178.4 3.0 %fusion.35 = f32[1,4096,128]{2,1,0:T(8,128)S(1)} fusion(f32[512,4096]{1,0:T(8,128)S(1)} %get-tuple-element.154, f32[4096]{0:T(1024)S(1)} %bitcast.73, s32[4096]{0:T(1024)S(1)} %bitcast.82, s32[512]{0:T(512)S(1)} %bitcast.94, f32[1,4096,128]{2,1,0:T(8,128)S(1)} %copy-done.1, f32[4096]{0:T(1024)S(1)} %bitcast.91, pred[]{:T(512)S(6)} %compare.3, ...), kind=kOutput, calls=%fused_computation.7.clone.1 | convolution fusion | flops 548929536 | bytes 12765185 | tf_op jit(solution)/shard_map/while/body/eval_jaxpr/goi,ogt->git/dot_general | solution.py:57
  187.5 3.0 %fusion.35 = f32[1,4096,128]{2,1,0:T(8,128)S(1)} fusion(f32[512,4096]{1,0:T(8,128)S(1)} %get-tuple-element.154, f32[4096]{0:T(1024)S(1)} %bitcast.73, s32[4096]{0:T(1024)S(1)} %bitcast.82, s32[512]{0:T(512)S(1)} %bitcast.94, f32[1,4096,128]{2,1,0:T(8,128)S(1)} %copy-done.1, f32[4096]{0:T(1024)S(1)} %bitcast.91, pred[]{:T(512)S(6)} %compare.3, ...), kind=kOutput, calls=%fused_computation.7.clone.1 | convolution fusion | flops 548929536 | bytes 12765185 | tf_op jit(solution)/shard_map/while/body/eval_jaxpr/goi,ogt->git/dot_general | solution.py:57
  205.6 3.0 %fusion.35 = f32[1,4096,128]{2,1,0:T(8,128)S(1)} fusion(f32[512,4096]{1,0:T(8,128)S(1)} %get-tuple-element.154, f32[4096]{0:T(1024)S(1)} %bitcast.73, s32[4096]{0:T(1024)S(1)} %bitcast.82, s32[512]{0:T(512)S(1)} %bitcast.94, f32[1,4096,128]{2,1,0:T(8,128)S(1)} %copy-done.1, f32[4096]{0:T(1024)S(1)} %bitcast.91, pred[]{:T(512)S(6)} %compare.3, ...), kind=kOutput, calls=%fused_computation.7.clone.1 | convolution fusion | flops 548929536 | bytes 12765185 | tf_op jit(solution)/shard_map/while/body/eval_jaxpr/goi,ogt->git/dot_general | solution.py:57
  214.6 3.0 %fusion.35 = f32[1,4096,128]{2,1,0:T(8,128)S(1)} fusion(f32[512,4096]{1,0:T(8,128)S(1)} %get-tuple-element.154, f32[4096]{0:T(1024)S(1)} %bitcast.73, s32[4096]{0:T(1024)S(1)} %bitcast.82, s32[512]{0:T(512)S(1)} %bitcast.94, f32[1,4096,128]{2,1,0:T(8,128)S(1)} %copy-done.1, f32[4096]{0:T(1024)S(1)} %bitcast.91, pred[]{:T(512)S(6)} %compare.3, ...), kind=kOutput, calls=%fused_computation.7.clone.1 | convolution fusion | flops 548929536 | bytes 12765185 | tf_op jit(solution)/shard_map/while/body/eval_jaxpr/goi,ogt->git/dot_general | solution.py:57
  223.7 3.0 %fusion.35 = f32[1,4096,128]{2,1,0:T(8,128)S(1)} fusion(f32[512,4096]{1,0:T(8,128)S(1)} %get-tuple-element.154, f32[4096]{0:T(1024)S(1)} %bitcast.73, s32[4096]{0:T(1024)S(1)} %bitcast.82, s32[512]{0:T(512)S(1)} %bitcast.94, f32[1,4096,128]{2,1,0:T(8,128)S(1)} %copy-done.1, f32[4096]{0:T(1024)S(1)} %bitcast.91, pred[]{:T(512)S(6)} %compare.3, ...), kind=kOutput, calls=%fused_computation.7.clone.1 | convolution fusion | flops 548929536 | bytes 12765185 | tf_op jit(solution)/shard_map/while/body/eval_jaxpr/goi,ogt->git/dot_general | solution.py:57
  232.7 3.0 %fusion.35 = f32[1,4096,128]{2,1,0:T(8,128)S(1)} fusion(f32[512,4096]{1,0:T(8,128)S(1)} %get-tuple-element.154, f32[4096]{0:T(1024)S(1)} %bitcast.73, s32[4096]{0:T(1024)S(1)} %bitcast.82, s32[512]{0:T(512)S(1)} %bitcast.94, f32[1,4096,128]{2,1,0:T(8,128)S(1)} %copy-done.1, f32[4096]{0:T(1024)S(1)} %bitcast.91, pred[]{:T(512)S(6)} %compare.3, ...), kind=kOutput, calls=%fused_computation.7.clone.1 | convolution fusion | flops 548929536 | bytes 12765185 | tf_op jit(solution)/shard_map/while/body/eval_jaxpr/goi,ogt->git/dot_general | solution.py:57
  241.8 3.0 %fusion.35 = f32[1,4096,128]{2,1,0:T(8,128)S(1)} fusion(f32[512,4096]{1,0:T(8,128)S(1)} %get-tuple-element.154, f32[4096]{0:T(1024)S(1)} %bitcast.73, s32[4096]{0:T(1024)S(1)} %bitcast.82, s32[512]{0:T(512)S(1)} %bitcast.94, f32[1,4096,128]{2,1,0:T(8,128)S(1)} %copy-done.1, f32[4096]{0:T(1024)S(1)} %bitcast.91, pred[]{:T(512)S(6)} %compare.3, ...), kind=kOutput, calls=%fused_computation.7.clone.1 | convolution fusion | flops 548929536 | bytes 12765185 | tf_op jit(solution)/shard_map/while/body/eval_jaxpr/goi,ogt->git/dot_general | solution.py:57
  249.3 24.1 %all_to_all.55 = bf16[16,64,512]{2,1,0:T(8,128)(2,1)S(1)} all-to-all(bf16[16,64,512]{2,1,0:T(8,128)(2,1)S(1)} %convert_element_type.20), channel_id=1, replica_groups=mesh['outer_0'=4,'outer_1'=2,'inner'=16] {'inner'}, dimensions={0} | all-to-all | bytes 2097152 | tf_op jit(solution)/shard_map/all_to_all | solution.py:136
  (237 shorter events, 113.4 us)
Async XLA Ops:
  6.5 43.4 %all-gather.3.cloned.1.call-start = ((), (), s32[]{:S(2)}) async-start(), calls=%async_computation.4 | async-start | bytes 1572864 | tf_op jit(solution)/shard_map/all_gather | solution.py:36
  28.0 73.4 %all-gather.5.cloned.1.call-start = ((), (), s32[]{:S(2)}) async-start(), calls=%async_computation.5 | async-start | bytes 5242880 | tf_op jit(solution)/shard_map/all_gather | solution.py:36
  51.3 14.3 %all-to-all-start = ((s32[16,1,64]{2,1,0:T(1,128)}), s32[16,1,64]{2,1,0:T(1,128)S(1)}, u32[]{:S(2)}, u32[]{:S(2)}) async-start(s32[16,1,64]{2,1,0:T(1,128)} %broadcast_in_dim.35), calls=%async_computation | async-start | bytes 16384 | tf_op jit(solution)/shard_map/all_to_all | solution.py:25
  65.5 27.6 %all-to-all-start.2 = ((bf16[64,16,512]{2,0,1:T(8,128)(2,1)}), bf16[64,16,512]{2,0,1:T(8,128)(2,1)S(1)}, u32[]{:S(2)}, u32[]{:S(2)}) async-start(bf16[64,16,512]{2,0,1:T(8,128)(2,1)} %bitcast.50), calls=%async_computation.2 | async-start | bytes 2097152 | tf_op jit(solution)/shard_map/all_to_all | solution.py:113
  102.3 3.7 %copy-start.1 = (f32[1,4096,128]{2,1,0:T(8,128)S(1)}, f32[1,4096,128]{2,1,0:T(8,128)}, u32[]{:S(2)}) copy-start(f32[1,4096,128]{2,1,0:T(8,128)} %get-tuple-element.170) | copy-start | bytes 6291460 | tf_op jit(solution)/shard_map/while
  111.4 3.7 %copy-start.1 = (f32[1,4096,128]{2,1,0:T(8,128)S(1)}, f32[1,4096,128]{2,1,0:T(8,128)}, u32[]{:S(2)}) copy-start(f32[1,4096,128]{2,1,0:T(8,128)} %get-tuple-element.170) | copy-start | bytes 6291460 | tf_op jit(solution)/shard_map/while
  118.1 1.3 copy-start.2
  120.4 3.7 %copy-start.1 = (f32[1,4096,128]{2,1,0:T(8,128)S(1)}, f32[1,4096,128]{2,1,0:T(8,128)}, u32[]{:S(2)}) copy-start(f32[1,4096,128]{2,1,0:T(8,128)} %get-tuple-element.170) | copy-start | bytes 6291460 | tf_op jit(solution)/shard_map/while
  127.1 1.3 copy-start.2
  129.5 3.7 %copy-start.1 = (f32[1,4096,128]{2,1,0:T(8,128)S(1)}, f32[1,4096,128]{2,1,0:T(8,128)}, u32[]{:S(2)}) copy-start(f32[1,4096,128]{2,1,0:T(8,128)} %get-tuple-element.170) | copy-start | bytes 6291460 | tf_op jit(solution)/shard_map/while
  136.2 1.3 copy-start.2
  138.5 3.7 %copy-start.1 = (f32[1,4096,128]{2,1,0:T(8,128)S(1)}, f32[1,4096,128]{2,1,0:T(8,128)}, u32[]{:S(2)}) copy-start(f32[1,4096,128]{2,1,0:T(8,128)} %get-tuple-element.170) | copy-start | bytes 6291460 | tf_op jit(solution)/shard_map/while
  145.2 1.3 copy-start.2
  147.6 3.7 %copy-start.1 = (f32[1,4096,128]{2,1,0:T(8,128)S(1)}, f32[1,4096,128]{2,1,0:T(8,128)}, u32[]{:S(2)}) copy-start(f32[1,4096,128]{2,1,0:T(8,128)} %get-tuple-element.170) | copy-start | bytes 6291460 | tf_op jit(solution)/shard_map/while
  156.6 3.7 %copy-start.1 = (f32[1,4096,128]{2,1,0:T(8,128)S(1)}, f32[1,4096,128]{2,1,0:T(8,128)}, u32[]{:S(2)}) copy-start(f32[1,4096,128]{2,1,0:T(8,128)} %get-tuple-element.170) | copy-start | bytes 6291460 | tf_op jit(solution)/shard_map/while
  165.7 3.7 %copy-start.1 = (f32[1,4096,128]{2,1,0:T(8,128)S(1)}, f32[1,4096,128]{2,1,0:T(8,128)}, u32[]{:S(2)}) copy-start(f32[1,4096,128]{2,1,0:T(8,128)} %get-tuple-element.170) | copy-start | bytes 6291460 | tf_op jit(solution)/shard_map/while
  174.7 3.7 %copy-start.1 = (f32[1,4096,128]{2,1,0:T(8,128)S(1)}, f32[1,4096,128]{2,1,0:T(8,128)}, u32[]{:S(2)}) copy-start(f32[1,4096,128]{2,1,0:T(8,128)} %get-tuple-element.170) | copy-start | bytes 6291460 | tf_op jit(solution)/shard_map/while
  183.7 3.7 %copy-start.1 = (f32[1,4096,128]{2,1,0:T(8,128)S(1)}, f32[1,4096,128]{2,1,0:T(8,128)}, u32[]{:S(2)}) copy-start(f32[1,4096,128]{2,1,0:T(8,128)} %get-tuple-element.170) | copy-start | bytes 6291460 | tf_op jit(solution)/shard_map/while
  192.8 3.7 %copy-start.1 = (f32[1,4096,128]{2,1,0:T(8,128)S(1)}, f32[1,4096,128]{2,1,0:T(8,128)}, u32[]{:S(2)}) copy-start(f32[1,4096,128]{2,1,0:T(8,128)} %get-tuple-element.170) | copy-start | bytes 6291460 | tf_op jit(solution)/shard_map/while
  201.8 3.7 %copy-start.1 = (f32[1,4096,128]{2,1,0:T(8,128)S(1)}, f32[1,4096,128]{2,1,0:T(8,128)}, u32[]{:S(2)}) copy-start(f32[1,4096,128]{2,1,0:T(8,128)} %get-tuple-element.170) | copy-start | bytes 6291460 | tf_op jit(solution)/shard_map/while
  210.9 3.7 %copy-start.1 = (f32[1,4096,128]{2,1,0:T(8,128)S(1)}, f32[1,4096,128]{2,1,0:T(8,128)}, u32[]{:S(2)}) copy-start(f32[1,4096,128]{2,1,0:T(8,128)} %get-tuple-element.170) | copy-start | bytes 6291460 | tf_op jit(solution)/shard_map/while
  219.9 3.7 %copy-start.1 = (f32[1,4096,128]{2,1,0:T(8,128)S(1)}, f32[1,4096,128]{2,1,0:T(8,128)}, u32[]{:S(2)}) copy-start(f32[1,4096,128]{2,1,0:T(8,128)} %get-tuple-element.170) | copy-start | bytes 6291460 | tf_op jit(solution)/shard_map/while
  229.0 3.7 %copy-start.1 = (f32[1,4096,128]{2,1,0:T(8,128)S(1)}, f32[1,4096,128]{2,1,0:T(8,128)}, u32[]{:S(2)}) copy-start(f32[1,4096,128]{2,1,0:T(8,128)} %get-tuple-element.170) | copy-start | bytes 6291460 | tf_op jit(solution)/shard_map/while
  238.0 3.7 %copy-start.1 = (f32[1,4096,128]{2,1,0:T(8,128)S(1)}, f32[1,4096,128]{2,1,0:T(8,128)}, u32[]{:S(2)}) copy-start(f32[1,4096,128]{2,1,0:T(8,128)} %get-tuple-element.170) | copy-start | bytes 6291460 | tf_op jit(solution)/shard_map/while
  (13 other events, 16.8 us)
Sparse Core Ops, SparseCore 0:
  28.1 21.8 all-gather.2
  51.6 49.6 all-gather.4
where the time goes:
time: 282 us; the launch traced here: 281 us
  matrix products  70.2 us (25%)
  blocking collectives  66 us (23%)
  local copies, waits for them, and re-layouts  45.5 us (16%)
  other arithmetic  39 us (14%)
  waiting for transfers between devices  34.5 us (12%)
  between operations  13.5 us (5%)
  starting transfers between devices  11.3 us (4%)
    dot_general x16, matrix products, update(): jnp.einsum('goi,ogt->git', softmax_weights.astype(jnp.bfloat16), value_sl...  47.4 us
    reduce_sum x16, other arithmetic, update(): running_sum = running_sum * rescale + jnp.sum(softmax_weights, axis=1)  34.9 us
    all_gather x2, waiting for transfers between devices, gather_axes(): value = lax.all_gather(value, axis, axis=dim, tiled=True)  29.8 us
    all_to_all x1, blocking collectives, body(): lax.all_to_all(result, 'inner', split_axis=0, concat_axis=1, tiled=True)  24.1 us
    dot_general x16, matrix products, update(): jnp.einsum('lva,vga->vlg', key_slice, query_cluster, preferred_element_ty...  22.8 us
    all_gather x2, blocking collectives, gather_axes(): value = lax.all_gather(value, axis, axis=dim, tiled=True)  22.4 us
    while x112, local copies, waits for them, and re-layouts  21.2 us
    all_to_all x1, blocking collectives, body(): lax.all_to_all(kv_spread, 'inner', split_axis=1, concat_axis=0, tiled=True)  19.5 us
  transfers between devices with their start and end apart: 4, of which 3 were waited for; matrix products, arithmetic and copies ran while one was open for 2% of the time, Pallas kernels for 0%

commit v1 on v0

v1 whole, which is shorter than its diff:
```python
import functools, math
import jax
import jax.numpy as jnp
from jax import lax
from jax.experimental import pallas as pl
from jax.sharding import Mesh
from jax.sharding import PartitionSpec as P
from jax.experimental.pallas import tpu as pltpu

HEAD_WIDTH = 128
VMEM = pltpu.VMEM
LOW_TOP = -1e29
MASKED = -1e30
QT = 16
KT = 16

def f32(x): return x.astype(jnp.float32)
def b16(x): return x.astype(jnp.bfloat16)

def order_kernel(r0, r1, r2, r3, key_ref, val_ref, fwd_ref, back_ref):
    r = jnp.concatenate([r0[...], r1[...], r2[...], r3[...]], axis=0)
    n = r.shape[0]
    digits = f32(r[:, 256:384])
    pcol = digits[:, 0:1] * 64.0 + digits[:, 1:2]
    dt = digits.T
    prow = dt[0:1, :] * 64.0 + dt[1:2, :]
    below = jnp.where(pcol < prow, 1.0, 0.0)
    rank_row = jnp.sum(below, axis=0, keepdims=True)
    above = jnp.where(prow < pcol, 1.0, 0.0)
    rank_col = jnp.sum(above, axis=1, keepdims=True)
    rows = f32(lax.broadcasted_iota(jnp.int32, (n, n), 0))
    cols = f32(lax.broadcasted_iota(jnp.int32, (n, n), 1))
    fwd = b16(jnp.where(rows == rank_row, 1.0, 0.0))
    fwd_ref[...] = fwd
    back_ref[...] = b16(jnp.where(cols == rank_col, 1.0, 0.0))
    srt = jnp.dot(fwd, r, preferred_element_type=jnp.float32)
    key_ref[0:n, :] = b16(srt[:, 0:128])
    val_ref[...] = b16(srt[:, 128:256])
    st = srt[:, 256:384].T
    parts = [st[d:d + 1, 128 * c:128 * (c + 1)] for d in (0, 1) for c in range(n // 128)]
    parts.append(jnp.zeros((16 - len(parts), 128), jnp.float32))
    key_ref[n:n + 16, :] = b16(jnp.concatenate(parts, axis=0))

def order(pieces):
    n = 4 * pieces[0].shape[0]
    return pl.pallas_call(
        order_kernel,
        out_shape=(jax.ShapeDtypeStruct((n + 16, 128), jnp.bfloat16),
                   jax.ShapeDtypeStruct((n, 128), jnp.bfloat16),
                   jax.ShapeDtypeStruct((n, n), jnp.bfloat16),
                   jax.ShapeDtypeStruct((n, n), jnp.bfloat16)),
        name="order",
    )(*pieces)

def block_positions(dig, n):
    c = n // 128
    hi = jnp.concatenate([dig[:, i, :] for i in range(c)], axis=1)
    lo = jnp.concatenate([dig[:, c + i, :] for i in range(c)], axis=1)
    return hi, lo

def attend_kernel(heads, n, key_at, val_at, *refs):
    blocks = len(key_at)
    nk = 1 + max(a for a, _ in key_at)
    nv = 1 + max(a for a, _ in val_at)
    q0, q1, q2, q3, own_ref, fwd_ref, back_ref = refs[:7]
    key_refs, val_refs = refs[7:7 + nk], refs[7 + nk:7 + nk + nv]
    (out_ref, vt_ref, kp_ref, qs_ref, os_ref, qp_ref, acc_ref, qhl_ref, s0_ref, s1_ref, p0_ref, p1_ref, bounds) = refs[7 + nk + nv:]
    def key_rows(start, count):
        return [key_refs[a][j, pl.ds(start, count), :] for a, j in key_at]
    def val_rows(start, count):
        return [val_refs[a][j, pl.ds(start, count), :] for a, j in val_at]
    dv = HEAD_WIDTH
    ntile = n // KT
    qtiles = n // QT
    width = KT * blocks
    qw = QT * heads
    scale = math.log2(math.e) / math.sqrt(dv)
    for c in range(heads * dv // 512):
        qs_ref[:, 512 * c:512 * (c + 1)] = b16(jnp.dot(fwd_ref[...], jnp.concatenate([q[:, 512 * c:512 * (c + 1)] for q in (q0, q1, q2, q3)], axis=0), preferred_element_type=jnp.float32))
    hi, lo = block_positions(f32(jnp.stack(key_rows(n, 16))), n)
    kpos = hi * 64.0 + lo
    kcol = kpos.T
    for t in range(ntile):
        slab = kcol[KT * t:KT * (t + 1), :]
        for b in range(blocks):
            kp_ref[t, KT * b:KT * (b + 1), :] = jnp.broadcast_to(slab[:, b:b + 1], (KT, 128))
        v = jnp.concatenate(val_rows(KT * t, KT), axis=0)
        vt_ref[t, 0:dv, :] = b16(f32(v).T)
        vt_ref[t, dv:dv + 16, :] = jnp.ones((16, width), jnp.bfloat16)
    low = jnp.min(kpos, axis=0, keepdims=True)
    high = jnp.max(kpos, axis=0, keepdims=True)
    lane = lax.broadcasted_iota(jnp.int32, (1, n), 1)
    own_hi, own_lo = block_positions(f32(own_ref[n:n + 16, :])[None], n)
    tile_of = lax.broadcasted_iota(jnp.int32, (qtiles, n), 1) // QT
    mine = tile_of == lax.broadcasted_iota(jnp.int32, (qtiles, n), 0)
    rep = b16(jnp.where(lax.broadcasted_iota(jnp.int32, (n, qw), 0) % QT == lax.broadcasted_iota(jnp.int32, (n, qw), 1) % QT, 1.0, 0.0))
    mh = b16(jnp.where(mine, own_hi, 0.0))
    ml = b16(jnp.where(mine, own_lo, 0.0))
    qp_ref[0:qtiles, :] = (jnp.dot(mh, rep, preferred_element_type=jnp.float32) * 64.0
                   + jnp.dot(ml, rep, preferred_element_type=jnp.float32))
    own = own_hi * 64.0 + own_lo
    for i in range(qtiles):
        first = own[:, QT * i:QT * i + 1]
        last = own[:, QT * i + QT - 1:QT * i + QT]
        seen = jnp.where((lane % KT == 0) & (low <= last), 1.0, 0.0)
        full = jnp.where((lane % KT == KT - 1) & (high <= first), 1.0, 0.0)
        bounds[0, i] = jnp.sum(full).astype(jnp.int32)
        bounds[1, i] = jnp.sum(seen).astype(jnp.int32)

    for i in range(qtiles):
        q = f32(qs_ref[QT * i:QT * (i + 1), :])
        qstack = jnp.concatenate([q[:, dv * h:dv * (h + 1)] for h in range(heads)], axis=0)
        qt = qstack.T * scale
        qhi = b16(qt)
        qhl_ref[i, 0:dv, :] = qhi
        qhl_ref[i, dv:2 * dv, :] = b16(qt - f32(qhi))
    acc_ref[...] = jnp.zeros_like(acc_ref)
    p1_ref[...] = jnp.zeros_like(p1_ref)

    def score(i, t, s_ref):
        k = jnp.concatenate(key_rows(pl.multiple_of(t * KT, KT), KT), axis=0)
        kk = jnp.concatenate([k, k], axis=1)
        s_ref[...] = jnp.dot(kk, qhl_ref[i], preferred_element_type=jnp.float32)

    def soft(i, t, top, s_ref, p_ref):
        kp = kp_ref[t]
        vis = jnp.concatenate([kp] * (qw // 128), axis=1) <= qp_ref[pl.ds(i, 1), :]
        s = jnp.where(vis, s_ref[...], MASKED)
        top = jnp.where(t == 0, LOW_TOP, top)
        new = jnp.maximum(top, jnp.max(s, axis=0, keepdims=True))
        p_ref[...] = b16(jnp.exp2(s - new))
        return new, jnp.where(t == 0, 0.0, jnp.exp2(top - new))

    def gather(i, t, alpha, p_ref):
        pv = jnp.dot(vt_ref[t], p_ref[...], preferred_element_type=jnp.float32)
        acc_ref[i] = acc_ref[i] * alpha + pv

    def after(i, t):
        more = t + 1 < bounds[1, jnp.minimum(i, qtiles - 1)]
        return jnp.where(i >= qtiles, i, jnp.where(more, i, i + 1)), jnp.where(i >= qtiles, 0, jnp.where(more, t + 1, 0))

    score(0, 0, s0_ref)
    total = bounds[1, 0]
    for i in range(1, qtiles):
        total = total + bounds[1, i]

    def pair(w, carry):
        pi, pt, ci, ct, top, alpha = carry
        ni, nt = after(ci, ct)
        score(ni, nt, s1_ref)
        gather(pi, pt, alpha, p1_ref)
        top, alpha = soft(ci, ct, top, s0_ref, p0_ref)
        ei, et = after(ni, nt)
        score(ei, et, s0_ref)
        gather(ci, ct, alpha, p0_ref)
        top, alpha = soft(ni, nt, top, s1_ref, p1_ref)
        return ni, nt, ei, et, top, alpha

    z = jnp.int32(0)
    pi, pt, ci, ct, top, alpha = lax.fori_loop(0, (total + 1) // 2, pair, (
        jnp.int32(qtiles), z, z, z, jnp.full((1, qw), LOW_TOP, jnp.float32), jnp.zeros((1, qw), jnp.float32)))
    gather(pi, pt, alpha, p1_ref)
    for i in range(qtiles):
        o = acc_ref[i, 0:dv, :] / acc_ref[i, dv:dv + 1, :]
        ot = o.T
        os_ref[QT * i:QT * (i + 1), :] = b16(jnp.concatenate([ot[QT * h:QT * (h + 1), :] for h in range(heads)], axis=1))

    for c in range(heads * dv // 512):
        out_ref[:, 512 * c:512 * (c + 1)] = b16(jnp.dot(back_ref[...], os_ref[:, 512 * c:512 * (c + 1)], preferred_element_type=jnp.float32))

def attend(qs, own, fwd, back, key_arrays, val_arrays, key_at, val_at):
    n, hw = fwd.shape[0], qs[0].shape[1]
    heads = hw // HEAD_WIDTH
    blocks = len(key_at)
    qw = QT * heads
    ntile = n // KT
    return pl.pallas_call(
        functools.partial(attend_kernel, heads, n, key_at, val_at),
        out_shape=jax.ShapeDtypeStruct((n, hw), jnp.bfloat16),
        scratch_shapes=[
            VMEM((ntile, HEAD_WIDTH + 16, KT * blocks), jnp.bfloat16),
            VMEM((ntile, KT * blocks, 128), jnp.float32),
            VMEM((n, hw), jnp.bfloat16),
            VMEM((n, hw), jnp.bfloat16),
            VMEM((n // QT + 8, qw), jnp.float32),
            VMEM((n // QT + 1, HEAD_WIDTH + 16, qw), jnp.float32),
            VMEM((n // QT + 1, 2 * HEAD_WIDTH, qw), jnp.bfloat16),
            VMEM((KT * blocks, qw), jnp.float32),
            VMEM((KT * blocks, qw), jnp.float32),
            VMEM((KT * blocks, qw), jnp.bfloat16),
            VMEM((KT * blocks, qw), jnp.bfloat16),
            pltpu.SMEM((2, n // QT), jnp.int32),
        ],
        compiler_params=pltpu.CompilerParams(vmem_limit_bytes=48 * 1024 * 1024),
        name="attend",
        cost_estimate=pl.CostEstimate(flops=2 * 2 * n * heads * blocks * n * HEAD_WIDTH, bytes_accessed=8 << 20, transcendentals=n * heads * blocks * n),
    )(*qs, own, fwd, back, *key_arrays, *val_arrays)

AXES = ("z", "xlo", "y", "xhi", "c")
XAXES = ("xlo", "xhi")

def x_index(x):
    return (x % 2) * 2 + x // 2

def shift(value, axis, by):
    if axis == "x":
        return lax.ppermute(value, XAXES, [(x_index(i), x_index((i + by) % 4)) for i in range(4)])
    size = lax.axis_size(axis)
    return lax.ppermute(value, axis, [(i, (i + by) % size) for i in range(size)])

def gather_row(value, axis):
    return jnp.stack([value, shift(value, axis, 1), shift(value, axis, 3), shift(value, axis, 2)])

def gather_wide(value, axis):
    right, left = shift(value, axis, 1), shift(value, axis, 3)
    far_a, far_b = shift(right[:2], axis, 1), shift(left[2:], axis, 3)
    return jnp.concatenate([value, right, left, far_a, far_b])

def body(query_proj, key_proj, value_proj, positions):
    rows, width = query_proj.shape
    me = lax.axis_index("y")
    group = width // 4
    digits = jnp.stack([positions // 64, positions % 64], axis=1).astype(jnp.bfloat16)
    digits = jnp.pad(digits, ((0, 0), (0, HEAD_WIDTH - 2)))
    pack = jnp.stack([jnp.concatenate([key_proj[:, HEAD_WIDTH * h:HEAD_WIDTH * (h + 1)],
                                       value_proj[:, HEAD_WIDTH * h:HEAD_WIDTH * (h + 1)], digits], axis=1) for h in range(4)])
    def for_peer(by):
        return lax.dynamic_index_in_dim(pack, (me + by) % 4, 0, keepdims=False)
    pieces = [for_peer(0)] + [shift(for_peer(by), "y", by) for by in (1, 2, 3)]
    def q_for(by):
        return lax.dynamic_slice_in_dim(query_proj, ((me + by) % 4) * group, group, 1)
    qs = [q_for(0)] + [shift(q_for(by), "y", by) for by in (1, 2, 3)]
    key, val, fwd, back = order(pieces)
    key_all = gather_wide(gather_row(key, "z"), "x")
    val_all = gather_wide(gather_row(val, "x"), "z")
    key_twin, val_twin = shift(key_all, "c", 1), shift(val_all, "c", 1)
    key_at, val_at = [], []
    for core in range(2):
        for dx in range(4):
            for dz in range(4):
                key_at.append((core, 4 * dx + dz))
                val_at.append((core, 4 * dz + dx))
    out = attend(qs, key, fwd, back, [key_all, key_twin], [val_all, val_twin], key_at, val_at)
    back_home = [out[0:rows]] + [shift(out[rows * by:rows * (by + 1)], "y", 4 - by) for by in (1, 2, 3)]
    stacked = jnp.stack(back_home)
    result = jnp.concatenate([lax.dynamic_index_in_dim(stacked, (h - me) % 4, 0, keepdims=False) for h in range(4)], axis=1)
    return result

def solution(mesh):
    finer = Mesh(mesh.devices.reshape(4, 2, 4, 2, 2), AXES)
    return jax.shard_map(
        body,
        mesh=finer,
        in_specs=(P(AXES, None), P(AXES, None), P(AXES, None), P(AXES)),
        out_specs=P(AXES, None),
        check_vma=False,
    )
```

time: 282 us -> 131 us (0.46)
  matrix products: 70.2 us -> 0 us
  blocking collectives: 66 us -> 0 us
  Pallas kernels: 0 us -> 45.5 us
  local copies, waits for them, and re-layouts: 45.5 us -> 7.77 us
  other arithmetic: 39 us -> 2.96 us
  starting transfers between devices: 11.3 us -> 39.9 us
  between operations: 13.5 us -> 0.34 us
    dot_general x32 -> x0, matrix products: 70.2 us -> none  [the longest x16 47.4 us: update(): jnp.einsum('goi,ogt->git', softmax_weights.astype(jnp.bfloat16), value_sl...]
    pallas_call x0 -> x2, Pallas kernels: none -> 45.5 us  [the longest x1 43.5 us: attend(): pl.pallas_call(functools.partial(attend_kernel, heads, n, key_at, val_at)...]
    all_to_all x2 -> x0, blocking collectives: 43.6 us -> none  [the longest x1 24.1 us: body(): lax.all_to_all(result, 'inner', split_axis=0, concat_axis=1, tiled=True)]
    ppermute x0 -> x25, starting transfers between devices: none -> 39.9 us  [the longest x18 30.1 us: shift(): lax.ppermute(value, axis, [(i, (i + by) % size) for i in range(size)])]
    reduce_sum x16 -> x0, other arithmetic: 34.9 us -> none  [update(): running_sum = running_sum * rescale + jnp.sum(softmax_weights, axis=1)]
    ppermute x0 -> x25, waiting for transfers between devices: none -> 32.2 us  [the longest x18 28.7 us: shift(): lax.ppermute(value, axis, [(i, (i + by) % size) for i in range(size)])]
    all_gather x2 -> x0, waiting for transfers between devices: 29.8 us -> none  [gather_axes(): value = lax.all_gather(value, axis, axis=dim, tiled=True)]
    all_gather x2 -> x0, blocking collectives: 22.4 us -> none  [gather_axes(): value = lax.all_gather(value, axis, axis=dim, tiled=True)]
  transfers between devices with their start and end apart: 4 -> 25, of which waited for: 3 -> 9; matrix products, arithmetic and copies ran while one was open for 2% -> 4% of each run, Pallas kernels for 0% -> 0%
where the time goes in v1:
time: 131 us; the launch traced here: 129 us
  Pallas kernels  45.5 us (35%)
  starting transfers between devices  39.9 us (30%)
  waiting for transfers between devices  32.2 us (25%)
  local copies, waits for them, and re-layouts  7.77 us (6%)
  other arithmetic  2.96 us (2%)
    pallas_call x1, Pallas kernels, attend(): pl.pallas_call(functools.partial(attend_kernel, heads, n, key_at, val_at)...  43.5 us
    ppermute x18, starting transfers between devices, shift(): lax.ppermute(value, axis, [(i, (i + by) % size) for i in range(size)])  30.1 us
    ppermute x18, waiting for transfers between devices, shift(): lax.ppermute(value, axis, [(i, (i + by) % size) for i in range(size)])  28.7 us
    ppermute x7, starting transfers between devices, shift(): lax.ppermute(value, XAXES, [(x_index(i), x_index((i + by) % 4)) for i in...  9.76 us
    unnamed x34, local copies, waits for them, and re-layouts  3.62 us
    ppermute x7, waiting for transfers between devices, shift(): lax.ppermute(value, XAXES, [(x_index(i), x_index((i + by) % 4)) for i in...  3.44 us
  transfers between devices with their start and end apart: 25, of which 9 were waited for; matrix products, arithmetic and copies ran while one was open for 4% of the time, Pallas kernels for 0%

profile of v1, /device:TPU:1, one launch (start us, length us, event | category | flops | bytes accessed | tf_op | source)
XLA Modules:
  0.0 128.6 jit_solution(17364622003417960331)
XLA Ops:
  3.6 2.2 %collective-permute-start.3 = (bf16[64,384]{1,0:T(8,128)(2,1)S(1)}, bf16[64,384]{1,0:T(8,128)(2,1)S(1)}, u32[]{:S(2)}, u32[]{:S(2)}) collective-permute-start(bf16[64,384]{1,0:T(8,128)(2,1)S(1)} %bitcast.57), channel_id=1, source_target_pairs={{0,4},{4,8},{8,12},{12,0},{1,5},{5,9},{9,13},{13,1},{2,6},{6,10},{... | collective-permute-start | bytes 147464 | tf_op jit(solution)/shard_map/ppermute | solution.py:209
  5.9 2.7 %collective-permute-start.4 = (bf16[64,384]{1,0:T(8,128)(2,1)S(1)}, bf16[64,384]{1,0:T(8,128)(2,1)S(1)}, u32[]{:S(2)}, u32[]{:S(2)}) collective-permute-start(bf16[64,384]{1,0:T(8,128)(2,1)S(1)} %bitcast.58), channel_id=1, source_target_pairs={{0,8},{4,12},{8,0},{12,4},{1,9},{5,13},{9,1},{13,5},{2,10},{6,14},... | collective-permute-start | bytes 147464 | tf_op jit(solution)/shard_map/ppermute | solution.py:209
  10.5 1.4 %collective-permute-done.5.r3 = bf16[64,384]{1,0:T(8,128)(2,1)S(1)} collective-permute-done((bf16[64,384]{1,0:T(8,128)(2,1)S(1)}, bf16[64,384]{1,0:T(8,128)(2,1)S(1)}, u32[]{:S(2)}, u32[]{:S(2)}) %collective-permute-start.5) | collective-permute-done | bytes 49184 | tf_op jit(solution)/shard_map/ppermute | solution.py:209
  12.6 2.0 %order.1 = (bf16[272,128]{1,0:T(8,128)(2,1)}, bf16[256,128]{1,0:T(8,128)(2,1)}, bf16[256,256]{1,0:T(8,128)(2,1)}, bf16[256,256]{1,0:T(8,128)(2,1)}) custom-call(bf16[64,384]{1,0:T(8,128)(2,1)} %bitcast.56, bf16[64,384]{1,0:T(8,128)(2,1)} %copy-done.3, bf16[64,384]{1,0:T(8,128)(2,1)} %copy-done.4, bf16[64,384]{1,0:T(8,128)(2,1)} %copy-done.5), custom_call_target="tpu_custom_call" | custom-call | tf_op jit(solution)/shard_map/order/pallas_call | solution.py:46
  14.6 1.2 collective-permute-start.14
  15.8 1.5 %collective-permute-start.15 = (bf16[256,128]{1,0:T(8,128)(2,1)}, bf16[256,128]{1,0:T(8,128)(2,1)S(1)}, u32[]{:S(2)}, u32[]{:S(2)}) collective-permute-start(bf16[256,128]{1,0:T(8,128)(2,1)} %get-tuple-element.12), channel_id=1, source_target_pairs={{0,18},{16,0},{2,16},{18,2},{1,19},{17,1},{3,17},{19,3},{4,22},{20... | collective-permute-start | bytes 196616 | tf_op jit(solution)/shard_map/ppermute | solution.py:207
  17.3 1.5 %collective-permute-start.16 = (bf16[256,128]{1,0:T(8,128)(2,1)}, bf16[256,128]{1,0:T(8,128)(2,1)S(1)}, u32[]{:S(2)}, u32[]{:S(2)}) collective-permute-start(bf16[256,128]{1,0:T(8,128)(2,1)} %get-tuple-element.12), channel_id=1, source_target_pairs={{0,2},{16,18},{2,0},{18,16},{1,3},{17,19},{3,1},{19,17},{4,6},{20,... | collective-permute-start | bytes 196616 | tf_op jit(solution)/shard_map/ppermute | solution.py:207
  18.8 1.6 %collective-permute-start.6 = (bf16[272,128]{1,0:T(8,128)(2,1)}, bf16[272,128]{1,0:T(8,128)(2,1)S(1)}, u32[]{:S(2)}, u32[]{:S(2)}) collective-permute-start(bf16[272,128]{1,0:T(8,128)(2,1)} %get-tuple-element.9.refs_4_), channel_id=1, source_target_pairs={{0,32},{32,64},{64,96},{96,0},{1,33},{33,65},{65,97},{97,1},{2,34}... | collective-permute-start | bytes 208904 | tf_op jit(solution)/shard_map/ppermute | solution.py:209
  22.2 2.1 %collective-permute-start.7 = (bf16[272,128]{1,0:T(8,128)(2,1)}, bf16[272,128]{1,0:T(8,128)(2,1)S(1)}, u32[]{:S(2)}, u32[]{:S(2)}) collective-permute-start(bf16[272,128]{1,0:T(8,128)(2,1)} %get-tuple-element.9.refs_4_), channel_id=1, source_target_pairs={{0,96},{32,0},{64,32},{96,64},{1,97},{33,1},{65,33},{97,65},{2,98}... | collective-permute-start | bytes 208904 | tf_op jit(solution)/shard_map/ppermute | solution.py:209
  24.3 1.3 %collective-permute-start.8 = (bf16[272,128]{1,0:T(8,128)(2,1)}, bf16[272,128]{1,0:T(8,128)(2,1)S(1)}, u32[]{:S(2)}, u32[]{:S(2)}) collective-permute-start(bf16[272,128]{1,0:T(8,128)(2,1)} %get-tuple-element.9.refs_4_), channel_id=1, source_target_pairs={{0,64},{32,96},{64,0},{96,32},{1,65},{33,97},{65,1},{97,33},{2,66}... | collective-permute-start | bytes 208904 | tf_op jit(solution)/shard_map/ppermute | solution.py:209
  27.3 1.9 %collective-permute-start.18 = (bf16[4,256,128]{2,1,0:T(8,128)(2,1)S(1)}, bf16[4,256,128]{2,1,0:T(8,128)(2,1)S(1)}, u32[]{:S(2)}, u32[]{:S(2)}) collective-permute-start(bf16[4,256,128]{2,1,0:T(8,128)(2,1)S(1)} %pad_maximum_fusion.4), channel_id=1, source_target_pairs={{0,96},{32,0},{64,32},{96,64},{1,97},{33,1},{65,33},{97,65},{2,98}... | collective-permute-start | bytes 786440 | tf_op jit(solution)/shard_map/ppermute | solution.py:209
  30.2 2.4 %collective-permute-start.10 = (bf16[4,272,128]{2,1,0:T(8,128)(2,1)S(1)}, bf16[4,272,128]{2,1,0:T(8,128)(2,1)S(1)}, u32[]{:S(2)}, u32[]{:S(2)}) collective-permute-start(bf16[4,272,128]{2,1,0:T(8,128)(2,1)S(1)} %pad_maximum_fusion.3), channel_id=1, source_target_pairs={{0,18},{16,0},{2,16},{18,2},{1,19},{17,1},{3,17},{19,3},{4,22},{20... | collective-permute-start | bytes 835592 | tf_op jit(solution)/shard_map/ppermute | solution.py:207
  33.9 2.7 %collective-permute-start.20 = (bf16[2,256,128]{2,1,0:T(8,128)(2,1)S(1)}, bf16[2,256,128]{2,1,0:T(8,128)(2,1)S(1)}, u32[]{:S(2)}, u32[]{:S(2)}) collective-permute-start(bf16[2,256,128]{2,1,0:T(8,128)(2,1)S(1)} %slice.67), channel_id=1, source_target_pairs={{0,96},{32,0},{64,32},{96,64},{1,97},{33,1},{65,33},{97,65},{2,98}... | collective-permute-start | bytes 393224 | tf_op jit(solution)/shard_map/ppermute | solution.py:209
  37.1 2.5 %collective-permute-start.12 = (bf16[2,272,128]{2,1,0:T(8,128)(2,1)S(1)}, bf16[2,272,128]{2,1,0:T(8,128)(2,1)S(1)}, u32[]{:S(2)}, u32[]{:S(2)}) collective-permute-start(bf16[2,272,128]{2,1,0:T(8,128)(2,1)S(1)} %slice.65), channel_id=1, source_target_pairs={{0,18},{16,0},{2,16},{18,2},{1,19},{17,1},{3,17},{19,3},{4,22},{20... | collective-permute-start | bytes 417800 | tf_op jit(solution)/shard_map/ppermute | solution.py:207
  39.8 3.3 %collective-permute-done.11 = bf16[2,272,128]{2,1,0:T(8,128)(2,1)S(1)} collective-permute-done((bf16[2,272,128]{2,1,0:T(8,128)(2,1)S(1)}, bf16[2,272,128]{2,1,0:T(8,128)(2,1)S(1)}, u32[]{:S(2)}, u32[]{:S(2)}) %collective-permute-start.11) | collective-permute-done | bytes 139296 | tf_op jit(solution)/shard_map/ppermute | solution.py:207
  43.2 6.1 %collective-permute-start.13 = (bf16[16,272,128]{2,1,0:T(8,128)(2,1)S(1)}, bf16[16,272,128]{2,1,0:T(8,128)(2,1)}, u32[]{:S(2)}, u32[]{:S(2)}) collective-permute-start(bf16[16,272,128]{2,1,0:T(8,128)(2,1)S(1)} %constant_dynamic-update-slice_fusion.refs_7_), channel_id=1, source_target_pairs={{0,1},{1,0},{2,3},{3,2},{4,5},{5,4},{6,7},{7,6},{8,9},{9,8},{10,11... | collective-permute-start | bytes 3342344 | tf_op jit(solution)/shard_map/ppermute | solution.py:209
  49.5 1.3 %constant_dynamic-slice_fusion.4 = (bf16[64,2048]{1,0:T(8,128)(2,1)S(1)}, bf16[64,2048]{1,0:T(8,128)(2,1)S(1)}, bf16[64,2048]{1,0:T(8,128)(2,1)S(1)}, bf16[64,2048]{1,0:T(8,128)(2,1)S(1)}) fusion(bf16[64,8192]{1,0:T(8,128)(2,1)} %param.4, s32[]{:T(128)S(6)} %select_n.99, s32[]{:T(128)S(6)} %select_n.95, s32[]{:T(128)S(6)} %select_n.93, s32[]{:T(128)S(6)} %select_n.97), kind=kLoop, calls=%fused_computation.42 | loop fusion | bytes 2097168 | tf_op jit(solution)/shard_map/dynamic_slice | solution.py:231
  50.8 3.4 %collective-permute-start.1 = (bf16[64,2048]{1,0:T(8,128)(2,1)S(1)}, bf16[64,2048]{1,0:T(8,128)(2,1)S(1)}, u32[]{:S(2)}, u32[]{:S(2)}) collective-permute-start(bf16[64,2048]{1,0:T(8,128)(2,1)S(1)} %get-tuple-element.24), channel_id=1, source_target_pairs={{0,8},{4,12},{8,0},{12,4},{1,9},{5,13},{9,1},{13,5},{2,10},{6,14},... | collective-permute-start | bytes 786440 | tf_op jit(solution)/shard_map/ppermute | solution.py:209
  54.3 5.2 %collective-permute-done.refs_1_ = bf16[64,2048]{1,0:T(8,128)(2,1)S(1)} collective-permute-done((bf16[64,2048]{1,0:T(8,128)(2,1)S(1)}, bf16[64,2048]{1,0:T(8,128)(2,1)S(1)}, u32[]{:S(2)}, u32[]{:S(2)}) %collective-permute-start) | collective-permute-done | bytes 262176 | tf_op jit(solution)/shard_map/ppermute | solution.py:209
  59.5 6.4 %collective-permute-done.1.refs_2_ = bf16[64,2048]{1,0:T(8,128)(2,1)S(1)} collective-permute-done((bf16[64,2048]{1,0:T(8,128)(2,1)S(1)}, bf16[64,2048]{1,0:T(8,128)(2,1)S(1)}, u32[]{:S(2)}, u32[]{:S(2)}) %collective-permute-start.1) | collective-permute-done | bytes 262176 | tf_op jit(solution)/shard_map/ppermute | solution.py:209
  65.9 43.5 %attend.1 = bf16[256,2048]{1,0:T(8,128)(2,1)S(1)} custom-call(bf16[64,2048]{1,0:T(8,128)(2,1)S(1)} %get-tuple-element.23.refs_0_, bf16[64,2048]{1,0:T(8,128)(2,1)S(1)} %collective-permute-done.refs_1_, bf16[64,2048]{1,0:T(8,128)(2,1)S(1)} %collective-permute-done.1.refs_2_, bf16[64,2048]{1,0:T(8,128)(2,1)S(1)} %collective-permute-done.2.refs_3_, ...), custom_call_target="tpu_custom_call" | custom-call | flops 17179869184 | bytes 8388608 | tf_op jit(solution)/shard_map/attend/pallas_call | solution.py:177
  109.4 3.1 %collective-permute-start.22 = (bf16[64,2048]{1,0:T(8,128)(2,1)S(1)}, bf16[64,2048]{1,0:T(8,128)(2,1)S(1)}, u32[]{:S(2)}, u32[]{:S(2)}) collective-permute-start(bf16[64,2048]{1,0:T(8,128)(2,1)S(1)} %get-tuple-element.20), channel_id=1, source_target_pairs={{0,12},{4,0},{8,4},{12,8},{1,13},{5,1},{9,5},{13,9},{2,14},{6,2},{... | collective-permute-start | bytes 786440 | tf_op jit(solution)/shard_map/ppermute | solution.py:209
  113.2 11.1 %collective-permute-done.22 = bf16[64,2048]{1,0:T(8,128)(2,1)S(1)} collective-permute-done((bf16[64,2048]{1,0:T(8,128)(2,1)S(1)}, bf16[64,2048]{1,0:T(8,128)(2,1)S(1)}, u32[]{:S(2)}, u32[]{:S(2)}) %collective-permute-start.22) | collective-permute-done | bytes 262176 | tf_op jit(solution)/shard_map/ppermute | solution.py:209
  124.3 3.0 %collective-permute-done.24 = bf16[64,2048]{1,0:T(8,128)(2,1)S(1)} collective-permute-done((bf16[64,2048]{1,0:T(8,128)(2,1)S(1)}, bf16[64,2048]{1,0:T(8,128)(2,1)S(1)}, u32[]{:S(2)}, u32[]{:S(2)}) %collective-permute-start.24) | collective-permute-done | bytes 262176 | tf_op jit(solution)/shard_map/ppermute | solution.py:209
  (86 shorter events, 14.7 us)
Async XLA Ops:
  3.6 6.9 %collective-permute-start.3 = (bf16[64,384]{1,0:T(8,128)(2,1)S(1)}, bf16[64,384]{1,0:T(8,128)(2,1)S(1)}, u32[]{:S(2)}, u32[]{:S(2)}) collective-permute-start(bf16[64,384]{1,0:T(8,128)(2,1)S(1)} %bitcast.57), channel_id=1, source_target_pairs={{0,4},{4,8},{8,12},{12,0},{1,5},{5,9},{9,13},{13,1},{2,6},{6,10},{... | collective-permute-start | bytes 147464 | tf_op jit(solution)/shard_map/ppermute | solution.py:209
  5.9 4.7 %collective-permute-start.4 = (bf16[64,384]{1,0:T(8,128)(2,1)S(1)}, bf16[64,384]{1,0:T(8,128)(2,1)S(1)}, u32[]{:S(2)}, u32[]{:S(2)}) collective-permute-start(bf16[64,384]{1,0:T(8,128)(2,1)S(1)} %bitcast.58), channel_id=1, source_target_pairs={{0,8},{4,12},{8,0},{12,4},{1,9},{5,13},{9,1},{13,5},{2,10},{6,14},... | collective-permute-start | bytes 147464 | tf_op jit(solution)/shard_map/ppermute | solution.py:209
  14.6 9.7 %collective-permute-start.14 = (bf16[256,128]{1,0:T(8,128)(2,1)}, bf16[256,128]{1,0:T(8,128)(2,1)S(1)}, u32[]{:S(2)}, u32[]{:S(2)}) collective-permute-start(bf16[256,128]{1,0:T(8,128)(2,1)} %get-tuple-element.12), channel_id=1, source_target_pairs={{0,16},{16,2},{2,18},{18,0},{1,17},{17,3},{3,19},{19,1},{4,20},{20... | collective-permute-start | bytes 196616 | tf_op jit(solution)/shard_map/ppermute | solution.py:207
  15.8 9.8 %collective-permute-start.15 = (bf16[256,128]{1,0:T(8,128)(2,1)}, bf16[256,128]{1,0:T(8,128)(2,1)S(1)}, u32[]{:S(2)}, u32[]{:S(2)}) collective-permute-start(bf16[256,128]{1,0:T(8,128)(2,1)} %get-tuple-element.12), channel_id=1, source_target_pairs={{0,18},{16,0},{2,16},{18,2},{1,19},{17,1},{3,17},{19,3},{4,22},{20... | collective-permute-start | bytes 196616 | tf_op jit(solution)/shard_map/ppermute | solution.py:207
  17.3 8.4 %collective-permute-start.16 = (bf16[256,128]{1,0:T(8,128)(2,1)}, bf16[256,128]{1,0:T(8,128)(2,1)S(1)}, u32[]{:S(2)}, u32[]{:S(2)}) collective-permute-start(bf16[256,128]{1,0:T(8,128)(2,1)} %get-tuple-element.12), channel_id=1, source_target_pairs={{0,2},{16,18},{2,0},{18,16},{1,3},{17,19},{3,1},{19,17},{4,6},{20,... | collective-permute-start | bytes 196616 | tf_op jit(solution)/shard_map/ppermute | solution.py:207
  18.8 10.5 %collective-permute-start.6 = (bf16[272,128]{1,0:T(8,128)(2,1)}, bf16[272,128]{1,0:T(8,128)(2,1)S(1)}, u32[]{:S(2)}, u32[]{:S(2)}) collective-permute-start(bf16[272,128]{1,0:T(8,128)(2,1)} %get-tuple-element.9.refs_4_), channel_id=1, source_target_pairs={{0,32},{32,64},{64,96},{96,0},{1,33},{33,65},{65,97},{97,1},{2,34}... | collective-permute-start | bytes 208904 | tf_op jit(solution)/shard_map/ppermute | solution.py:209
  22.2 7.1 %collective-permute-start.7 = (bf16[272,128]{1,0:T(8,128)(2,1)}, bf16[272,128]{1,0:T(8,128)(2,1)S(1)}, u32[]{:S(2)}, u32[]{:S(2)}) collective-permute-start(bf16[272,128]{1,0:T(8,128)(2,1)} %get-tuple-element.9.refs_4_), channel_id=1, source_target_pairs={{0,96},{32,0},{64,32},{96,64},{1,97},{33,1},{65,33},{97,65},{2,98}... | collective-permute-start | bytes 208904 | tf_op jit(solution)/shard_map/ppermute | solution.py:209
  24.3 5.5 %collective-permute-start.8 = (bf16[272,128]{1,0:T(8,128)(2,1)}, bf16[272,128]{1,0:T(8,128)(2,1)S(1)}, u32[]{:S(2)}, u32[]{:S(2)}) collective-permute-start(bf16[272,128]{1,0:T(8,128)(2,1)} %get-tuple-element.9.refs_4_), channel_id=1, source_target_pairs={{0,64},{32,96},{64,0},{96,32},{1,65},{33,97},{65,1},{97,33},{2,66}... | collective-permute-start | bytes 208904 | tf_op jit(solution)/shard_map/ppermute | solution.py:209
  26.5 7.2 %collective-permute-start.17 = (bf16[4,256,128]{2,1,0:T(8,128)(2,1)S(1)}, bf16[4,256,128]{2,1,0:T(8,128)(2,1)S(1)}, u32[]{:S(2)}, u32[]{:S(2)}) collective-permute-start(bf16[4,256,128]{2,1,0:T(8,128)(2,1)S(1)} %pad_maximum_fusion.4), channel_id=1, source_target_pairs={{0,32},{32,64},{64,96},{96,0},{1,33},{33,65},{65,97},{97,1},{2,34}... | collective-permute-start | bytes 786440 | tf_op jit(solution)/shard_map/ppermute | solution.py:209
  27.3 6.5 %collective-permute-start.18 = (bf16[4,256,128]{2,1,0:T(8,128)(2,1)S(1)}, bf16[4,256,128]{2,1,0:T(8,128)(2,1)S(1)}, u32[]{:S(2)}, u32[]{:S(2)}) collective-permute-start(bf16[4,256,128]{2,1,0:T(8,128)(2,1)S(1)} %pad_maximum_fusion.4), channel_id=1, source_target_pairs={{0,96},{32,0},{64,32},{96,64},{1,97},{33,1},{65,33},{97,65},{2,98}... | collective-permute-start | bytes 786440 | tf_op jit(solution)/shard_map/ppermute | solution.py:209
  29.8 7.0 %collective-permute-start.9 = (bf16[4,272,128]{2,1,0:T(8,128)(2,1)S(1)}, bf16[4,272,128]{2,1,0:T(8,128)(2,1)S(1)}, u32[]{:S(2)}, u32[]{:S(2)}) collective-permute-start(bf16[4,272,128]{2,1,0:T(8,128)(2,1)S(1)} %pad_maximum_fusion.3), channel_id=1, source_target_pairs={{0,16},{16,2},{2,18},{18,0},{1,17},{17,3},{3,19},{19,1},{4,20},{20... | collective-permute-start | bytes 835592 | tf_op jit(solution)/shard_map/ppermute | solution.py:207
  30.2 6.9 %collective-permute-start.10 = (bf16[4,272,128]{2,1,0:T(8,128)(2,1)S(1)}, bf16[4,272,128]{2,1,0:T(8,128)(2,1)S(1)}, u32[]{:S(2)}, u32[]{:S(2)}) collective-permute-start(bf16[4,272,128]{2,1,0:T(8,128)(2,1)S(1)} %pad_maximum_fusion.3), channel_id=1, source_target_pairs={{0,18},{16,0},{2,16},{18,2},{1,19},{17,1},{3,17},{19,3},{4,22},{20... | collective-permute-start | bytes 835592 | tf_op jit(solution)/shard_map/ppermute | solution.py:207
  33.8 6.0 %collective-permute-start.19 = (bf16[2,256,128]{2,1,0:T(8,128)(2,1)S(1)}, bf16[2,256,128]{2,1,0:T(8,128)(2,1)S(1)}, u32[]{:S(2)}, u32[]{:S(2)}) collective-permute-start(bf16[2,256,128]{2,1,0:T(8,128)(2,1)S(1)} %slice.66), channel_id=1, source_target_pairs={{0,32},{32,64},{64,96},{96,0},{1,33},{33,65},{65,97},{97,1},{2,34}... | collective-permute-start | bytes 393224 | tf_op jit(solution)/shard_map/ppermute | solution.py:209
  33.9 15.4 %collective-permute-start.20 = (bf16[2,256,128]{2,1,0:T(8,128)(2,1)S(1)}, bf16[2,256,128]{2,1,0:T(8,128)(2,1)S(1)}, u32[]{:S(2)}, u32[]{:S(2)}) collective-permute-start(bf16[2,256,128]{2,1,0:T(8,128)(2,1)S(1)} %slice.67), channel_id=1, source_target_pairs={{0,96},{32,0},{64,32},{96,64},{1,97},{33,1},{65,33},{97,65},{2,98}... | collective-permute-start | bytes 393224 | tf_op jit(solution)/shard_map/ppermute | solution.py:209
  36.8 6.3 %collective-permute-start.11 = (bf16[2,272,128]{2,1,0:T(8,128)(2,1)S(1)}, bf16[2,272,128]{2,1,0:T(8,128)(2,1)S(1)}, u32[]{:S(2)}, u32[]{:S(2)}) collective-permute-start(bf16[2,272,128]{2,1,0:T(8,128)(2,1)S(1)} %slice.64), channel_id=1, source_target_pairs={{0,16},{16,2},{2,18},{18,0},{1,17},{17,3},{3,19},{19,1},{4,20},{20... | collective-permute-start | bytes 417800 | tf_op jit(solution)/shard_map/ppermute | solution.py:207
  37.1 6.0 %collective-permute-start.12 = (bf16[2,272,128]{2,1,0:T(8,128)(2,1)S(1)}, bf16[2,272,128]{2,1,0:T(8,128)(2,1)S(1)}, u32[]{:S(2)}, u32[]{:S(2)}) collective-permute-start(bf16[2,272,128]{2,1,0:T(8,128)(2,1)S(1)} %slice.65), channel_id=1, source_target_pairs={{0,18},{16,0},{2,16},{18,2},{1,19},{17,1},{3,17},{19,3},{4,22},{20... | collective-permute-start | bytes 417800 | tf_op jit(solution)/shard_map/ppermute | solution.py:207
  43.2 22.7 %collective-permute-start.13 = (bf16[16,272,128]{2,1,0:T(8,128)(2,1)S(1)}, bf16[16,272,128]{2,1,0:T(8,128)(2,1)}, u32[]{:S(2)}, u32[]{:S(2)}) collective-permute-start(bf16[16,272,128]{2,1,0:T(8,128)(2,1)S(1)} %constant_dynamic-update-slice_fusion.refs_7_), channel_id=1, source_target_pairs={{0,1},{1,0},{2,3},{3,2},{4,5},{5,4},{6,7},{7,6},{8,9},{9,8},{10,11... | collective-permute-start | bytes 3342344 | tf_op jit(solution)/shard_map/ppermute | solution.py:209
  49.3 16.5 %collective-permute-start.21 = (bf16[16,256,128]{2,1,0:T(8,128)(2,1)S(1)}, bf16[16,256,128]{2,1,0:T(8,128)(2,1)S(1)}, u32[]{:S(2)}, u32[]{:S(2)}) collective-permute-start(bf16[16,256,128]{2,1,0:T(8,128)(2,1)S(1)} %constant_dynamic-update-slice_fusion.8.refs_9_), channel_id=1, source_target_pairs={{0,1},{1,0},{2,3},{3,2},{4,5},{5,4},{6,7},{7,6},{8,9},{9,8},{10,11... | collective-permute-start | bytes 3145736 | tf_op jit(solution)/shard_map/ppermute | solution.py:209
  50.8 8.7 %collective-permute-start = (bf16[64,2048]{1,0:T(8,128)(2,1)S(1)}, bf16[64,2048]{1,0:T(8,128)(2,1)S(1)}, u32[]{:S(2)}, u32[]{:S(2)}) collective-permute-start(bf16[64,2048]{1,0:T(8,128)(2,1)S(1)} %get-tuple-element.22), channel_id=1, source_target_pairs={{0,4},{4,8},{8,12},{12,0},{1,5},{5,9},{9,13},{13,1},{2,6},{6,10},{... | collective-permute-start | bytes 786440 | tf_op jit(solution)/shard_map/ppermute | solution.py:209
  50.8 15.0 %collective-permute-start.1 = (bf16[64,2048]{1,0:T(8,128)(2,1)S(1)}, bf16[64,2048]{1,0:T(8,128)(2,1)S(1)}, u32[]{:S(2)}, u32[]{:S(2)}) collective-permute-start(bf16[64,2048]{1,0:T(8,128)(2,1)S(1)} %get-tuple-element.24), channel_id=1, source_target_pairs={{0,8},{4,12},{8,0},{12,4},{1,9},{5,13},{9,1},{13,5},{2,10},{6,14},... | collective-permute-start | bytes 786440 | tf_op jit(solution)/shard_map/ppermute | solution.py:209
  54.3 11.6 %collective-permute-start.2 = (bf16[64,2048]{1,0:T(8,128)(2,1)S(1)}, bf16[64,2048]{1,0:T(8,128)(2,1)S(1)}, u32[]{:S(2)}, u32[]{:S(2)}) collective-permute-start(bf16[64,2048]{1,0:T(8,128)(2,1)S(1)} %get-tuple-element.21), channel_id=1, source_target_pairs={{0,12},{4,0},{8,4},{12,8},{1,13},{5,1},{9,5},{13,9},{2,14},{6,2},{... | collective-permute-start | bytes 786440 | tf_op jit(solution)/shard_map/ppermute | solution.py:209
  109.4 14.8 %collective-permute-start.22 = (bf16[64,2048]{1,0:T(8,128)(2,1)S(1)}, bf16[64,2048]{1,0:T(8,128)(2,1)S(1)}, u32[]{:S(2)}, u32[]{:S(2)}) collective-permute-start(bf16[64,2048]{1,0:T(8,128)(2,1)S(1)} %get-tuple-element.20), channel_id=1, source_target_pairs={{0,12},{4,0},{8,4},{12,8},{1,13},{5,1},{9,5},{13,9},{2,14},{6,2},{... | collective-permute-start | bytes 786440 | tf_op jit(solution)/shard_map/ppermute | solution.py:209
  112.5 11.7 %collective-permute-start.23 = (bf16[64,2048]{1,0:T(8,128)(2,1)S(1)}, bf16[64,2048]{1,0:T(8,128)(2,1)S(1)}, u32[]{:S(2)}, u32[]{:S(2)}) collective-permute-start(bf16[64,2048]{1,0:T(8,128)(2,1)S(1)} %get-tuple-element.19), channel_id=1, source_target_pairs={{0,8},{4,12},{8,0},{12,4},{1,9},{5,13},{9,1},{13,5},{2,10},{6,14},... | collective-permute-start | bytes 786440 | tf_op jit(solution)/shard_map/ppermute | solution.py:209
  112.5 14.8 %collective-permute-start.24 = (bf16[64,2048]{1,0:T(8,128)(2,1)S(1)}, bf16[64,2048]{1,0:T(8,128)(2,1)S(1)}, u32[]{:S(2)}, u32[]{:S(2)}) collective-permute-start(bf16[64,2048]{1,0:T(8,128)(2,1)S(1)} %get-tuple-element.18), channel_id=1, source_target_pairs={{0,4},{4,8},{8,12},{12,0},{1,5},{5,9},{9,13},{13,1},{2,6},{6,10},{... | collective-permute-start | bytes 786440 | tf_op jit(solution)/shard_map/ppermute | solution.py:209
  (7 other events, 55.2 us)
